TPU v7x, 32 devices: a whole 2x2x4 slice. The times are simulated.
32 devices in a mesh: grp: 4 (over y, x), smp: 8 (over z, core).
Axes of the slice: x: 2, y: 2, z: 4, core: 2. Of those that a mesh axis runs over, the one named last changes fastest.
Arguments:
- spins_packed: int32 [32, 8192], P(None, 'smp'), may hold values from -2147483648 to 2147483646
- weight: bfloat16 [1024, 8192], P(None, 'grp'), may hold values from -0.1875 to 0.1875
- hidden_bias: float32 [8192], P('grp'), may hold values from -1.5 to 1.5
- force_w: float32 [1024, 8192], P('smp', 'grp'), may hold values from -6 to 6
- force_b: float32 [8192], P('grp'), may hold values from -6 to 6
Outputs:
- update_w: float32 [1024, 8192], P('smp', 'grp')
- update_b: float32 [8192], P('grp')
All inputs are finite; a program needn't handle non-finite values.
Results may differ from a plain program's by a relative error of at most 0.0003.
Values sent between devices are 32-bit elements; how exact they have to be, the bound alone decides.
A program may use at most 64 MiB of HBM per device.

v0:
```python
import jax
import jax.numpy as jnp
from jax import lax
from jax.sharding import PartitionSpec as P

ITERS = 2


diag_shift = 0.01


def unpack(packed):
    shifts = jnp.arange(32, dtype=jnp.int32)
    bit_values = jnp.bitwise_and(jnp.right_shift(packed[:, None, :], shifts[None, :, None]), 1)
    signs = 2 * bit_values - 1
    return signs.reshape(packed.shape[0] * 32, packed.shape[1]).astype(jnp.bfloat16)


def body(spins_packed, weight, hidden_bias, force_w, force_b):
    group_size = lax.axis_size("grp")
    shard_size = lax.axis_size("smp")
    spins = unpack(spins_packed)
    sample_count = spins.shape[1] * shard_size
    pre_activation = jnp.einsum("it,ih->th", spins, weight, preferred_element_type=jnp.float32)
    hidden = jnp.tanh(pre_activation + hidden_bias)

    def vector_dot(first_w, first_b, second_w, second_b):
        local_sum = jnp.sum(first_w * second_w) + jnp.sum(first_b * second_b) / shard_size
        return lax.psum(local_sum, ("grp", "smp"))

    solution_w = jnp.zeros_like(force_w)
    solution_b = jnp.zeros_like(force_b)
    residual_w, residual_b = (force_w, force_b)
    direction_w, direction_b = (force_w, force_b)
    norm_now = vector_dot(residual_w, residual_b, residual_w, residual_b)
    for iteration in range(ITERS):
        final_turn = iteration + 1 == ITERS
        projected = jnp.einsum(
            "it,ih->th",
            spins,
            lax.all_gather(direction_w, "smp", axis=0, tiled=True),
            precision=lax.Precision.HIGHEST,
            preferred_element_type=jnp.float32,
        )
        partial_value = jnp.sum(hidden * (projected + direction_b), axis=1)
        sample_values = lax.psum(partial_value, "grp")
        mean_value = lax.psum(jnp.sum(sample_values), "smp") / sample_count
        centred = sample_values - mean_value
        local_sum = jnp.sum(centred * centred) / (sample_count * group_size)
        local_sum = local_sum + diag_shift * (
            jnp.sum(direction_w * direction_w) + jnp.sum(direction_b * direction_b) / shard_size
        )
        curvature = lax.psum(local_sum, ("grp", "smp"))
        if not final_turn:
            scaled = centred / sample_count
            weighted = scaled[:, None] * hidden
            image_w = (
                lax.psum_scatter(
                    jnp.einsum(
                        "it,th->ih",
                        spins,
                        weighted,
                        precision=lax.Precision.HIGHEST,
                        preferred_element_type=jnp.float32,
                    ),
                    "smp",
                    scatter_dimension=0,
                    tiled=True,
                )
                + diag_shift * direction_w
            )
            bias_term = jnp.dot(
                scaled, hidden, precision=lax.Precision.HIGHEST, preferred_element_type=jnp.float32
            )
            image_b = lax.psum(bias_term, "smp") + diag_shift * direction_b
            image_w, image_b = (image_w, image_b)
        step_size = norm_now / curvature
        solution_w = solution_w + step_size * direction_w
        solution_b = solution_b + step_size * direction_b
        if not final_turn:
            residual_w = residual_w - step_size * image_w
            residual_b = residual_b - step_size * image_b
            norm_next = vector_dot(residual_w, residual_b, residual_w, residual_b)
            direction_w = residual_w + norm_next / norm_now * direction_w
            direction_b = residual_b + norm_next / norm_now * direction_b
            norm_now = norm_next
    return (solution_w, solution_b)


def solution(mesh):
    placed = (P(None, "smp"), P(None, "grp"), P("grp"), P("smp", "grp"), P("grp"))
    return jax.shard_map(
        body, mesh=mesh, in_specs=placed, out_specs=(P("smp", "grp"), P("grp")), check_vma=False
    )
```

profile of v0, /device:TPU:0, one launch (start us, length us, event | category | flops | bytes accessed | tf_op | source)
XLA Modules:
  0.0 464.2 jit_solution(10995732239375807882)
XLA Ops:
  7.2 0.7 all-gather.3.cloned.1.call-update
  8.0 0.1 shift_right_arithmetic.23
  8.0 1.7 fusion.6
  9.8 9.8 %fusion.10 = f32[1024,2048]{1,0:T(8,128)} fusion(bf16[1024,1024]{1,0:T(8,128)(2,1)S(1)} %fusion.6, bf16[1024,2048]{1,0:T(8,128)(2,1)} %param.6), kind=kOutput, calls=%fused_computation.29 | convolution fusion | flops 4294967296 | bytes 14680064 | tf_op jit(solution)/shard_map/it,ih->th/dot_general | solution.py:24
  19.6 74.8 %all-gather.3.cloned.1.call-done = f32[1024,2048]{1,0:T(8,128)} async-done(((f32[128,2048]{1,0:T(8,128)}), f32[1024,2048]{1,0:T(8,128)}) %all-gather.3.cloned.1.call-update) | async-done | bytes 8388624 | tf_op jit(solution)/shard_map/all_gather | solution.py:41
  94.4 18.4 %multiply_reduce_fusion.1 = f32[1024]{0:T(1024)S(1)} fusion(f32[1024,2048]{1,0:T(8,128)} %fusion.10, f32[2048]{0:T(1024)S(1)} %copy-done.3, f32[2048]{0:T(1024)S(1)} %copy-done.4, bf16[1024,1024]{1,0:T(8,128)(2,1)S(1)} %fusion.6, f32[1024,2048]{1,0:T(8,128)} %all-gather.3.cloned.1.call-done), kind=kOutput, calls=%fused_computation.3 | convolution fusion | flops 25778192384 | bytes 18894848 | tf_op jit(solution)/shard_map/it,ih->th/dot_general | solution.py:38
  112.8 9.9 %psum.64 = f32[1024]{0:T(1024)S(1)} all-reduce(f32[1024]{0:T(1024)S(1)} %multiply_reduce_fusion.1), channel_id=1, replica_groups=mesh['grp'=4,'smp'=8] {'grp'}, use_global_device_ids=true, to_apply=%region_4.0 | all-reduce | flops 1024 | bytes 8192 | tf_op jit(solution)/shard_map/psum | solution.py:46
  122.6 0.6 reduce_sum.119
  123.2 14.4 %psum.65 = f32[]{:T(128)} all-reduce(f32[]{:T(128)} %reduce_sum.119), channel_id=1, replica_groups=mesh['grp'=4,'smp'=8] {'smp'}, use_global_device_ids=true, to_apply=%region_6.0 | all-reduce | flops 1 | bytes 8 | tf_op jit(solution)/shard_map/psum | solution.py:47
  138.3 0.6 multiply_reduce_fusion.9
  138.9 17.6 %fusion = f32[1024,2048]{1,0:T(8,128)} fusion(bf16[1024,1024]{1,0:T(8,128)(2,1)S(1)} %fusion.6, f32[1024,2048]{1,0:T(8,128)} %fusion.10, f32[1024]{0:T(1024)S(1)} %get-tuple-element.9, f32[2048]{0:T(1024)S(1)} %copy-done.4), kind=kOutput, calls=%fused_computation.1 | convolution fusion | flops 25773998080 | bytes 18886656 | tf_op jit(solution)/shard_map/it,th->ih/dot_general | solution.py:59
  156.5 0.0 all-gather.5.cloned.1.call-start
  156.6 0.6 multiply_reduce_fusion.7
  157.8 0.9 multiply_reduce_fusion.4
  160.0 38.4 %all-reduce = (f32[]{:T(128)}, f32[]{:T(128)}) all-reduce(f32[]{:T(128)S(6)} %add.80, f32[]{:T(128)S(6)} %add.85), channel_id=1, replica_groups=mesh['grp'=4,'smp'=8] {'grp','smp'}, use_global_device_ids=true, to_apply=%region_2.0 | all-reduce | flops 2 | bytes 16 | tf_op jit(solution)/shard_map/psum | solution.py:29
  199.8 6.9 %fusion.2 = f32[1,2048]{1,0:T(1,128)S(1)} fusion(f32[1024,1]{0,1:T(1,128)S(1)} %bitcast.21, f32[1024,2048]{1,0:T(8,128)} %fusion.10, f32[2048]{0:T(1024)S(1)} %copy-done.4), kind=kOutput, calls=%fused_computation.5 | convolution fusion | flops 27262976 | bytes 8409088 | tf_op jit(solution)/shard_map/dot_general | solution.py:72
  206.6 16.9 %psum.67 = f32[2048]{0:T(1024)S(1)} all-reduce(f32[2048]{0:T(1024)S(1)} %bitcast.20), channel_id=1, replica_groups=mesh['grp'=4,'smp'=8] {'smp'}, use_global_device_ids=true, to_apply=%region_11.0 | all-reduce | flops 2048 | bytes 16384 | tf_op jit(solution)/shard_map/psum | solution.py:75
  223.5 0.6 multiply_reduce_fusion.6
  224.8 19.4 %reduce-scatter.2.cloned.1.call-done = f32[128,2048]{1,0:T(8,128)} async-done(((f32[1024,2048]{1,0:T(8,128)}), f32[128,2048]{1,0:T(8,128)}) %reduce-scatter.2.cloned.1.call-update) | async-done | bytes 1048592 | tf_op jit(solution)/shard_map/reduce_scatter | solution.py:58
  244.2 2.1 multiply_reduce_fusion.3
  247.0 38.0 %psum.68 = f32[]{:T(128)} all-reduce(f32[]{:T(128)S(6)} %add.88), channel_id=1, replica_groups=mesh['grp'=4,'smp'=8] {'grp','smp'}, use_global_device_ids=true, to_apply=%region_13.0 | all-reduce | flops 1 | bytes 8 | tf_op jit(solution)/shard_map/psum | solution.py:29
  286.3 3.1 multiply_reduce_fusion.2
  289.4 0.6 multiply_reduce_fusion.5
  291.3 80.9 %all-gather.5.cloned.1.call-done = f32[1024,2048]{1,0:T(8,128)} async-done(((f32[128,2048]{1,0:T(8,128)}), f32[1024,2048]{1,0:T(8,128)}) %all-gather.5.cloned.1.call-update) | async-done | bytes 8388624 | tf_op jit(solution)/shard_map/all_gather | solution.py:41
  372.2 19.0 %multiply_reduce_fusion = f32[1024]{0:T(1024)S(1)} fusion(f32[1024,2048]{1,0:T(8,128)} %fusion.10, f32[2048]{0:T(1024)S(1)} %get-tuple-element.5, f32[2048]{0:T(1024)S(1)} %copy-done.4, bf16[1024,1024]{1,0:T(8,128)(2,1)} %copy-done.2, f32[1024,2048]{1,0:T(8,128)} %all-gather.5.cloned.1.call-done), kind=kOutput, calls=%fused_computation | convolution fusion | flops 25778192384 | bytes 18894848 | tf_op jit(solution)/shard_map/it,ih->th/dot_general | solution.py:38
  391.2 9.9 %psum.69 = f32[1024]{0:T(1024)S(1)} all-reduce(f32[1024]{0:T(1024)S(1)} %multiply_reduce_fusion), channel_id=1, replica_groups=mesh['grp'=4,'smp'=8] {'grp'}, use_global_device_ids=true, to_apply=%region_15.0 | all-reduce | flops 1024 | bytes 8192 | tf_op jit(solution)/shard_map/psum | solution.py:46
  401.1 0.6 reduce_sum.124
  401.7 14.2 %psum.70 = f32[]{:T(128)} all-reduce(f32[]{:T(128)} %reduce_sum.124), channel_id=1, replica_groups=mesh['grp'=4,'smp'=8] {'smp'}, use_global_device_ids=true, to_apply=%region_17.0 | all-reduce | flops 1 | bytes 8 | tf_op jit(solution)/shard_map/psum | solution.py:47
  416.5 0.6 multiply_reduce_fusion.8
  417.8 36.8 %psum.71 = f32[]{:T(128)} all-reduce(f32[]{:T(128)S(6)} %add.94), channel_id=1, replica_groups=mesh['grp'=4,'smp'=8] {'grp','smp'}, use_global_device_ids=true, to_apply=%region_21.0 | all-reduce | flops 1 | bytes 8 | tf_op jit(solution)/shard_map/psum | solution.py:53
  455.9 0.6 multiply_add_fusion.2
  456.5 1.1 multiply_add_fusion
  (15 shorter events, 0.1 us)
Async XLA Ops:
  7.2 87.2 %all-gather.3.cloned.1.call-start = ((), (), s32[]{:S(2)}) async-start(), calls=%async_computation.1 | async-start | bytes 9437184 | tf_op jit(solution)/shard_map/all_gather | solution.py:41
  7.9 236.3 %reduce-scatter.2.cloned.1.call-start = ((), (), s32[]{:S(2)}) async-start(), calls=%async_computation.2 | async-start | bytes 9437184 | tf_op jit(solution)/shard_map/reduce_scatter | solution.py:58
  9.7 129.1 %copy-start.2 = (bf16[1024,1024]{1,0:T(8,128)(2,1)}, bf16[1024,1024]{1,0:T(8,128)(2,1)S(1)}, u32[]{:S(2)}) copy-start(bf16[1024,1024]{1,0:T(8,128)(2,1)S(1)} %fusion.6) | copy-start | bytes 6291460
  9.8 84.6 %copy-start.3 = (f32[2048]{0:T(1024)S(1)}, f32[2048]{0:T(1024)}, u32[]{:S(2)}) copy-start(f32[2048]{0:T(1024)} %param.9) | copy-start | bytes 24580
  9.8 84.6 %copy-start.4 = (f32[2048]{0:T(1024)S(1)}, f32[2048]{0:T(1024)}, u32[]{:S(2)}) copy-start(f32[2048]{0:T(1024)} %param.7) | copy-start | bytes 24580
  156.5 1.3 copy-start
  156.5 215.6 %all-gather.5.cloned.1.call-start = ((), (), s32[]{:S(2)}) async-start(), calls=%async_computation.3 | async-start | bytes 9437184 | tf_op jit(solution)/shard_map/all_gather | solution.py:41
  372.2 84.4 %copy-start.1 = (f32[128,2048]{1,0:T(8,128)S(1)}, f32[128,2048]{1,0:T(8,128)}, u32[]{:S(2)}) copy-start(f32[128,2048]{1,0:T(8,128)} %get-tuple-element.7) | copy-start | bytes 3145732
Sparse Core Ops, SparseCore 0:
  9.6 84.7 all-gather.2
  156.6 87.4 reduce-scatter.1
  289.5 82.6 all-gather.4
where the time goes:
time: 466 us; the launch traced here: 464 us
  blocking collectives  178 us (38%)
  waiting for transfers between devices  176 us (38%)
  matrix products  71.7 us (15%)
  between operations  24.3 us (5%)
  other arithmetic  13.8 us (3%)
    all_gather x2, waiting for transfers between devices, body(): lax.all_gather(direction_w, 'smp', axis=0, tiled=True)  156 us
    psum x2, blocking collectives, vector_dot(): return lax.psum(local_sum, ('grp', 'smp'))  76.4 us
    dot_general x2, matrix products, body(): jnp.einsum('it,ih->th', spins, lax.all_gather(direction_w, 'smp', axis=0,...  37.4 us
    psum x1, blocking collectives, body(): curvature = lax.psum(local_sum, ('grp', 'smp'))  36.8 us
    psum x2, blocking collectives, body(): mean_value = lax.psum(jnp.sum(sample_values), 'smp') / sample_count  28.6 us
    psum x2, blocking collectives, body(): sample_values = lax.psum(partial_value, 'grp')  19.7 us
    reduce_scatter x1, waiting for transfers between devices, body(): lax.psum_scatter(jnp.einsum('it,th->ih', spins, weighted, precision=lax.P...  19.4 us
    dot_general x1, matrix products, body(): jnp.einsum('it,th->ih', spins, weighted, precision=lax.Precision.HIGHEST,...  17.6 us
  transfers between devices with their start and end apart: 3, of which 3 were waited for; matrix products, arithmetic and copies ran while one was open for 5% of the time, Pallas kernels for 0%

commit v1 on v0

v1 whole, which is shorter than its diff:
```python
import functools

import jax
import jax.numpy as jnp
from jax import lax
from jax.experimental import pallas as pl
from jax.experimental.pallas import tpu as pltpu
from jax.sharding import PartitionSpec as P

MESH = pl.DeviceIdType.MESH
F32, BF16 = jnp.float32, jnp.bfloat16
diag_shift = 0.01
EXTRA = 128
PAD = 16


def total(x):
    return jnp.sum(jnp.sum(x, axis=0, keepdims=True), axis=1, keepdims=True)


def kernel(
    groups, shards,
    packed_ref, weight_ref, bias_ref, force_ref, force_b_ref,
    out_ref, out_b_ref,
    packed, weight_t, bias_t, tile, spins, hidden, force_other, lhs, scaled,
    image, image_other, residual, residual_b, by_group, by_shard,
    packed_send, packed_recv, force_sem, image_send, image_recv,
    group_send, group_recv, shard_send, shard_recv,
):
    grp, smp = lax.axis_index("grp"), lax.axis_index("smp")
    chips = shards // 2
    core, chip = lax.rem(smp, 2), smp // 2
    sibling = smp + 1 - 2 * core
    words, here = packed_ref.shape
    units, rows = weight_ref.shape[1], force_ref.shape[0]
    pair = 2 * rows
    samples = chips * here
    count = samples * 2
    block = hidden_block = min(512, units)
    part = image.shape[2]
    parts = units // part

    barrier = pltpu.get_barrier_semaphore()
    for step in range(1, groups):
        pl.semaphore_signal(barrier, device_id={"grp": lax.rem(grp + step, groups)}, device_id_type=MESH)
    for step in range(1, shards):
        pl.semaphore_signal(barrier, device_id={"smp": lax.rem(smp + step, shards)}, device_id_type=MESH)
    pl.semaphore_wait(barrier, groups + shards - 2)

    packed_copies = []
    for step in range(1, chips):
        peer = lax.rem(chip + step, chips)
        packed_copies.append(
            pltpu.make_async_remote_copy(
                packed_ref, packed.at[chip], packed_send.at[step], packed_recv.at[chip],
                device_id={"smp": 2 * peer + core}, device_id_type=MESH,
            )
        )
        packed_copies[-1].start()
    force_copy = pltpu.make_async_remote_copy(
        force_ref, force_other, force_sem.at[0], force_sem.at[1],
        device_id={"smp": sibling}, device_id_type=MESH,
    )
    force_copy.start()
    packed[chip] = packed_ref[...]

    def turn(at, carry):
        cols = pl.ds(pl.multiple_of(at * 256, 256), 256)
        weight_t[cols, :] = weight_ref[:, cols].T
        bias_t[cols, :] = jnp.broadcast_to(bias_ref[:, cols], (128, 256)).T
        return carry

    lax.fori_loop(0, units // 256, turn, 0)

    def own_rows(of):
        return pl.ds(pl.multiple_of(of * rows, rows), rows)

    zero_rows = jnp.zeros((PAD - 1, units), F32)
    lhs[pl.ds(pair, PAD), :] = jnp.concatenate([force_b_ref[...] / chips, zero_rows], axis=0).astype(BF16)
    lhs[own_rows(core), :] = force_ref[...].astype(BF16)
    force_copy.wait()
    lhs[own_rows(1 - core), :] = force_other[...].astype(BF16)

    shifts = lax.broadcasted_iota(jnp.int32, (32, block), 0)
    tiles = here // block

    def values_of(cols):
        projected = jnp.dot(lhs[...], hidden[:, cols], preferred_element_type=F32)
        value = jnp.sum(projected[:pair] * spins[:, cols].astype(F32), axis=0, keepdims=True)
        return value + projected[pair : pair + 1]

    def hidden_block_of(at_chip, turn_at, carry):
        local = pl.ds(pl.multiple_of(turn_at * block, block), block)
        cols = pl.ds(pl.multiple_of(at_chip * here + turn_at * block, block), block)
        for word in range(words):
            bits = jnp.right_shift(jnp.broadcast_to(packed[at_chip, word : word + 1, local], (32, block)), shifts)
            tile[word * 32 : word * 32 + 32, :] = (2 * jnp.bitwise_and(bits, 1) - 1).astype(F32).astype(BF16)
        spins[:, cols] = tile[pl.ds(pl.multiple_of(chip * pair, pair), pair), :]
        for unit in range(0, units, hidden_block):
            these = pl.ds(unit, hidden_block)
            pre = jnp.dot(weight_t[these, :], tile[...], preferred_element_type=F32)
            bias = bias_t[these, :]
            pre = pre + jnp.concatenate([bias] * (block // 128), axis=1)
            hidden[these, cols] = jnp.tanh(pre).astype(BF16)
        by_group[0, grp, :, cols] = values_of(cols)
        return carry

    for step in range(chips):
        at_chip = lax.rem(chip + chips - step, chips)
        if step:
            pltpu.make_async_remote_copy(
                packed_ref, packed.at[at_chip], packed_send.at[step], packed_recv.at[at_chip],
                device_id={"smp": sibling}, device_id_type=MESH,
            ).wait_recv()
        lax.fori_loop(0, tiles, functools.partial(hidden_block_of, at_chip), 0)
    for copy in packed_copies:
        copy.wait_send()

    def gather(slots, which, axis, size, me, send, recv):
        copies = []
        for step in range(1, size):
            copies.append(
                pltpu.make_async_remote_copy(
                    slots.at[which, me], slots.at[which, me], send.at[which, step], recv.at[which, me],
                    device_id={axis: lax.rem(me + step, size)}, device_id_type=MESH,
                )
            )
            copies[-1].start()
        for step in range(1, size):
            source = lax.rem(me + size - step, size)
            pltpu.make_async_remote_copy(
                slots.at[which, source], slots.at[which, source], send.at[which, step], recv.at[which, source],
                device_id={axis: source}, device_id_type=MESH,
            ).wait_recv()
        for copy in copies:
            copy.wait_send()

    lane = lax.broadcasted_iota(jnp.int32, (1, EXTRA), 1)

    def reduce_values(which, first, second):
        by_group[which, grp, :, samples:] = jnp.where(lane == 0, first, jnp.where(lane == 1, second, 0.0))
        gather(by_group, which, "grp", groups, grp, group_send, group_recv)
        mine = by_group[which, 0]
        for source in range(1, groups):
            mine = mine + by_group[which, source]
        by_shard[which, smp] = mine
        gather(by_shard, which, "smp", shards, smp, shard_send, shard_recv)
        halves = []
        for half in range(2):
            value = by_shard[which, half]
            for source in range(half + 2, shards, 2):
                value = value + by_shard[which, source]
            halves.append(value)
        extra = halves[0][:, samples:] + halves[1][:, samples:]
        first = jnp.sum(jnp.where(lane == 0, extra, 0.0), axis=1, keepdims=True)
        second = jnp.sum(jnp.where(lane == 1, extra, 0.0), axis=1, keepdims=True)
        return halves[0][:, :samples], halves[1][:, :samples], first, second

    def centre(low, high):
        mean = total(low) / count + total(high) / count
        return low - mean, high - mean

    force_dot = total(force_ref[...] * force_ref[...]) + total(force_b_ref[...] * force_b_ref[...]) / shards
    low0, high0, norm0, _ = reduce_values(0, force_dot, jnp.zeros((1, 1), F32))
    low, high = centre(low0, high0)
    curvature0 = total(low * low) / count + total(high * high) / count + diag_shift * norm0
    step0 = norm0 / curvature0

    mine = (jnp.where(core == 0, low, high)).astype(F32)
    for at in range(0, samples, block):
        weights = mine[:, at : at + block]
        scaled[:pair, at : at + block] = (spins[:, at : at + block].astype(F32) * weights).astype(BF16)
        scaled[pair:, at : at + block] = jnp.concatenate(
            [weights, jnp.zeros((PAD - 1, block), F32)], axis=0
        ).astype(BF16)

    def image_copy(at):
        return pltpu.make_async_remote_copy(
            image.at[at], image_other.at[at], image_send.at[at], image_recv.at[at],
            device_id={"smp": sibling}, device_id_type=MESH,
        )

    def image_part(at, carry):
        these = pl.ds(pl.multiple_of(at * part, part), part)
        image[at] = lax.dot_general(
            scaled[...], hidden[these, :], (((1,), (1,)), ((), ())), preferred_element_type=F32
        )
        image_copy(at).start()
        return carry

    lax.fori_loop(0, parts, image_part, 0)

    scale = 1.0 / count

    def residual_part(at, carry):
        first, second = carry
        these = pl.ds(pl.multiple_of(at * part, part), part)
        image_copy(at).wait()

        def next_residual(which, force):
            whole = image[at, which, :] + image_other[at, which, :]
            return force - step0 * (whole * scale + diag_shift * force)

        own = next_residual(own_rows(core), force_ref[:, these])
        residual[:, these] = own
        lhs[own_rows(core), these] = own.astype(BF16)
        lhs[own_rows(1 - core), these] = next_residual(own_rows(1 - core), force_other[:, these]).astype(BF16)
        own_b = next_residual(pl.ds(pair, 1), force_b_ref[:, these])
        residual_b[:, these] = own_b
        lhs[pl.ds(pair, PAD), these] = jnp.concatenate([own_b / chips, jnp.zeros((PAD - 1, part), F32)], axis=0).astype(BF16)
        first = first + total(own * own) + total(own_b * own_b) / shards
        second = second + total(own * force_ref[:, these]) + total(own_b * force_b_ref[:, these]) / shards
        return first, second

    zero = jnp.zeros((1, 1), F32)
    own_norm, own_cross = lax.fori_loop(0, parts, residual_part, (zero, zero))

    def second_values(at, carry):
        cols = pl.ds(pl.multiple_of(at * block, block), block)
        by_group[1, grp, :, cols] = values_of(cols)
        return carry

    lax.fori_loop(0, samples // block, second_values, 0)
    low1, high1, norm1, cross = reduce_values(1, own_norm, own_cross)
    beta = norm1 / norm0
    low, high = centre(low1 + beta * low0, high1 + beta * high0)
    direction_dot = norm1 + 2.0 * beta * cross + beta * beta * norm0
    curvature1 = total(low * low) / count + total(high * high) / count + diag_shift * direction_dot
    step1 = norm1 / curvature1

    out_ref[...] = step0 * force_ref[...] + step1 * (residual[...] + beta * force_ref[...])
    out_b_ref[...] = step0 * force_b_ref[...] + step1 * (residual_b[...] + beta * force_b_ref[...])


def body(groups, shards, spins_packed, weight, hidden_bias, force_w, force_b):
    words, here = spins_packed.shape
    inputs, units = weight.shape
    rows = force_w.shape[0]
    chips = shards // 2
    samples, pair = chips * here, 2 * rows
    part = 256
    parts = units // part
    vmem = pl.BlockSpec(memory_space=pltpu.VMEM)
    dma = pltpu.SemaphoreType.DMA
    update_w, update_b = pl.pallas_call(
        functools.partial(kernel, groups, shards),
        out_shape=(jax.ShapeDtypeStruct((rows, units), F32), jax.ShapeDtypeStruct((1, units), F32)),
        in_specs=[vmem] * 5,
        out_specs=(vmem, vmem),
        scratch_shapes=[
            pltpu.VMEM((chips, words, here), jnp.int32),
            pltpu.VMEM((units, inputs), BF16),
            pltpu.VMEM((units, 128), F32),
            pltpu.VMEM((inputs, min(512, units)), BF16),
            pltpu.VMEM((pair, samples), BF16),
            pltpu.VMEM((units, samples), BF16),
            pltpu.VMEM((rows, units), F32),
            pltpu.VMEM((pair + PAD, units), BF16),
            pltpu.VMEM((pair + PAD, samples), BF16),
            pltpu.VMEM((parts, pair + PAD, part), F32),
            pltpu.VMEM((parts, pair + PAD, part), F32),
            pltpu.VMEM((rows, units), F32),
            pltpu.VMEM((1, units), F32),
            pltpu.VMEM((2, groups, 1, samples + EXTRA), F32),
            pltpu.VMEM((2, shards, 1, samples + EXTRA), F32),
            dma((chips,)),
            dma((chips,)),
            dma((2,)),
            dma((parts,)),
            dma((parts,)),
            dma((2, groups)),
            dma((2, groups)),
            dma((2, shards)),
            dma((2, shards)),
        ],
        compiler_params=pltpu.CompilerParams(
            collective_id=0, has_side_effects=True, vmem_limit_bytes=62 * 1024 * 1024
        ),
    )(spins_packed, weight, hidden_bias.reshape(1, -1), force_w, force_b.reshape(1, -1))
    return update_w, update_b.reshape(-1)


def solution(mesh):
    placed = (P(None, "smp"), P(None, "grp"), P("grp"), P("smp", "grp"), P("grp"))
    return jax.shard_map(
        functools.partial(body, mesh.shape["grp"], mesh.shape["smp"]),
        mesh=mesh, in_specs=placed, out_specs=(P("smp", "grp"), P("grp")), check_vma=False,
    )
```

time: 466 us -> 70.9 us (0.15)
  blocking collectives: 178 us -> 0 us
  waiting for transfers between devices: 176 us -> 0 us
  matrix products: 71.7 us -> 0 us
  Pallas kernels: 0 us -> 66.4 us
  between operations: 24.3 us -> 0.64 us
  other arithmetic: 13.8 us -> 0 us
    psum x8 -> x0, blocking collectives: 178 us -> none  [the longest x2 76.4 us: vector_dot(): return lax.psum(local_sum, ('grp', 'smp'))]
    all_gather x2 -> x0, waiting for transfers between devices: 156 us -> none  [body(): lax.all_gather(direction_w, 'smp', axis=0, tiled=True)]
    dot_general x5 -> x0, matrix products: 71.7 us -> none  [the longest x2 37.4 us: body(): jnp.einsum('it,ih->th', spins, lax.all_gather(direction_w, 'smp', axis=0,...]
    pallas_call x0 -> x1, Pallas kernels: none -> 66.4 us  [body(): pl.pallas_call(functools.partial(kernel, groups, shards), out_shape=(jax....]
    reduce_scatter x1 -> x0, waiting for transfers between devices: 19.4 us -> none  [body(): lax.psum_scatter(jnp.einsum('it,th->ih', spins, weighted, precision=lax.P...]
    reduce_sum x10 -> x0, other arithmetic: 10.3 us -> none  [the longest x1 3.07 us: body(): jnp.sum(direction_w * direction_w)]
  transfers between devices with their start and end apart: 3 -> 0, of which waited for: 3 -> 0; matrix products, arithmetic and copies ran while one was open for 5% -> 0% of each run, Pallas kernels for 0% -> 0%
where the time goes in v1:
time: 70.9 us; the launch traced here: 70.7 us
  Pallas kernels  66.4 us (94%)
  local copies, waits for them, and re-layouts  3.59 us (5%)
    pallas_call x1, Pallas kernels, body(): pl.pallas_call(functools.partial(kernel, groups, shards), out_shape=(jax....  66.4 us
    unnamed x2, local copies, waits for them, and re-layouts  3.59 us

profile of v1, /device:TPU:0, one launch (start us, length us, event | category | flops | bytes accessed | tf_op | source)
XLA Modules:
  0.0 70.7 jit_solution(540424459916573371)
XLA Ops:
  0.6 66.4 %shard_map.68 = (f32[128,2048]{1,0:T(8,128)}, f32[1,2048]{1,0:T(1,128)}) custom-call(s32[32,1024]{1,0:T(8,128)} %packed_ref.1, bf16[1024,2048]{1,0:T(8,128)(2,1)} %weight_ref.1, f32[1,2048]{1,0:T(1,128)} %bitcast.3, f32[128,2048]{1,0:T(8,128)} %force_ref.1, f32[1,2048]{1,0:T(1,128)} %bitcast.4), custom_call_target="tpu_custom_call" | custom-call | tf_op jit(solution)/shard_map/pallas_call | solution.py:245
  67.1 2.3 %copy.9 = f32[128,2048]{1,0:T(8,128)} copy(f32[128,2048]{1,0:T(8,128)} %get-tuple-element.8) | data formatting | bytes 2097152
  69.4 1.3 %copy.10 = f32[2048]{0:T(1024)} copy(f32[2048]{0:T(1024)} %bitcast.5) | data formatting | bytes 16384
